TPU v7x, 16 devices: a whole 2x2x2 slice. The times are simulated.
16 devices in a mesh: dp: 2 (over z), tp: 8 (over y, x, core).
Axes of the slice: x: 2, y: 2, z: 2, core: 2. Of those that a mesh axis runs over, the one named last changes fastest.
Arguments:
- hidden: bfloat16 [4, 512, 2048], P('dp')
- targets: int32 [4, 512], P('dp')
- resp_mask: int32 [4, 512], P('dp')
- old_logp: float32 [4, 512], P('dp')
- advantages: float32 [4, 512], P('dp')
- gain: bfloat16 [2048], replicated
- w_head: bfloat16 [128256, 2048], P('tp')
Outputs:
- output 1: float32 [], replicated
- output 2: bfloat16 [4, 512, 2048], P('dp')
- output 3: float32 [128256, 2048], P(('tp', 'dp'))
- output 4: float32 [2048], replicated
All inputs are finite; a program needn't handle non-finite values.
Results may differ from a plain program's by a relative error of at most 0.001.
Values sent between devices are 32-bit elements.
A program may use at most 1 GiB of HBM per device.

v0:
```python
import jax
import jax.numpy as jnp
from jax import lax
from jax.sharding import PartitionSpec as P

EPSILON = 1e-5
CLIP_LOW = 0.8
CLIP_HIGH = 1.2
DUAL_CLIP = 3.0


def ppo_terms(logp, old_logp, advantages, tok_weight):
    prob_ratio = jnp.exp(logp - old_logp)
    loss_plain = -advantages * prob_ratio
    loss_clip = -advantages * jnp.clip(prob_ratio, CLIP_LOW, CLIP_HIGH)
    loss_max = jnp.maximum(loss_plain, loss_clip)
    dual_on = (advantages < 0) & (loss_max >= -DUAL_CLIP * advantages)
    tok_loss = jnp.where(dual_on, -DUAL_CLIP * advantages, loss_max)
    d_ratio = jnp.where(loss_plain >= loss_clip, -advantages, 0.0)
    d_ratio = jnp.where(dual_on, 0.0, d_ratio)
    return jnp.sum(tok_weight * tok_loss), tok_weight * d_ratio * prob_ratio


def solution(mesh):
    def local_step(hidden, targets, resp_mask, old_logp, advantages, gain, w_shard):
        row_count, seq_len, width = hidden.shape
        v_dev = w_shard.shape[0]
        n_tok = row_count * seq_len
        row_sums = jnp.sum(resp_mask, axis=1).astype(jnp.float32)
        rows_used = lax.psum(jnp.sum((row_sums > 0).astype(jnp.float32)), 'dp')
        tok_weight = (resp_mask.astype(jnp.float32) / jnp.maximum(row_sums, 1.0)[:, None] / rows_used).reshape(n_tok)
        h_float = hidden.reshape(n_tok, width).astype(jnp.float32)
        inv_rms = lax.rsqrt(jnp.mean(h_float * h_float, axis=-1, keepdims=True) + EPSILON)
        unit_rows = h_float * inv_rms
        x_act = (unit_rows * gain.astype(jnp.float32)).astype(jnp.bfloat16)
        logits = lax.dot_general(x_act, w_shard, (((1,), (1,)), ((), ())), preferred_element_type=jnp.float32)
        row_max = lax.pmax(jnp.max(logits, axis=-1), 'tp')
        local_ids = targets.reshape(n_tok) - lax.axis_index('tp') * v_dev
        is_target = lax.broadcasted_iota(jnp.int32, (1, v_dev), 1) == local_ids[:, None]
        part_stats = jnp.stack([jnp.sum(jnp.exp(logits - row_max[:, None]), axis=-1), jnp.sum(jnp.where(is_target, logits, 0.0), axis=-1)])
        tok_stats = lax.psum(part_stats, 'tp')
        log_norm = row_max + jnp.log(tok_stats[0])
        part_loss, d_logp = ppo_terms(tok_stats[1] - log_norm, old_logp.reshape(n_tok), advantages.reshape(n_tok), tok_weight)
        total_loss = lax.psum(part_loss, 'dp')
        soft_probs = jnp.exp(logits - log_norm[:, None])
        d_logits = (d_logp[:, None] * (jnp.where(is_target, 1.0, 0.0) - soft_probs)).astype(jnp.bfloat16)
        d_act = lax.psum(jnp.dot(d_logits, w_shard, preferred_element_type=jnp.float32), 'tp')
        head_part = lax.dot_general(d_logits, x_act, (((0,), (0,)), ((), ())), preferred_element_type=jnp.float32)
        d_head = lax.psum_scatter(head_part, 'dp', scatter_dimension=0, tiled=True)
        d_gain = lax.psum(jnp.sum(d_act * unit_rows, axis=0), 'dp')
        d_unit = d_act * gain.astype(jnp.float32)
        d_hidden = inv_rms * (d_unit - unit_rows * jnp.mean(d_unit * unit_rows, axis=-1, keepdims=True))
        return total_loss, d_hidden.astype(jnp.bfloat16).reshape(row_count, seq_len, width), d_head, d_gain

    row_spec = P('dp', None)
    return jax.shard_map(local_step, mesh=mesh, in_specs=(P('dp', None, None), row_spec, row_spec, row_spec, row_spec, P(None), P('tp', None)), out_specs=(P(), P('dp', None, None), P(('tp', 'dp'), None), P(None)), check_vma=False)
```

profile of v0, /device:TPU:0, one launch (start us, length us, event | category | flops | bytes accessed | tf_op | source)
XLA Modules:
  0.0 1747.3 jit_solution(14180379804113875694)
XLA Ops:
  8.0 0.0 all-reduce.4.cloned.1.call-start
  8.0 0.7 broadcast_compare_fusion
  8.7 0.7 negate_bitcast_fusion
  9.4 0.8 reduce_sum.72
  10.2 0.6 fusion
  10.8 6.8 psum.35
  17.7 0.6 maximum_multiply_fusion
  18.3 0.6 lt.13
  18.9 0.8 divide_bitcast_fusion
  19.7 0.6 copy.11
  20.3 0.7 subtract_bitcast_fusion
  21.0 1.3 copy.15
  22.3 3.1 multiply_reduce_fusion.2
  25.4 0.0 copy-start.3
  25.4 0.7 convert_element_type.41
  26.1 0.0 copy-start.1
  26.1 0.6 copy.12
  26.7 0.6 copy.16
  27.3 0.0 copy-done.3
  27.3 0.0 copy-done.1
  27.3 3.2 multiply_convert_fusion.2
  30.5 0.0 copy-start
  30.5 78.6 %fusion.3 = (f32[1024]{0:T(1024)S(1)}, f32[1024,16032]{0,1:T(8,128)}) fusion(bf16[1024,2048]{1,0:T(8,128)(2,1)S(1)} %multiply_convert_fusion.2, bf16[16032,2048]{1,0:T(8,128)(2,1)} %param.13), kind=kOutput, calls=%fused_computation.29 | convolution fusion | flops 67259498496 | bytes 135532544 | tf_op jit(solution)/shard_map/dot_general | solution.py:36
  109.1 0.0 copy-done
  109.1 13.1 pmax.7
  122.2 0.0 copy-start.5
  122.2 0.0 copy-start.7
  122.3 0.0 copy-start.9
  122.3 0.0 copy-start.11
  122.3 0.0 copy-start.15
  122.3 21.3 %exponential_reduce_fusion = (f32[1024]{0:T(1024)S(1)}, f32[1024]{0:T(1024)S(1)}) fusion(f32[1024,16032]{0,1:T(8,128)} %get-tuple-element.17, f32[1024]{0:T(1024)S(1)} %pmax.7, s32[1024]{0:T(1024)S(1)} %bitcast.53), kind=kLoop, calls=%fused_computation.3 | loop fusion | flops 82081792 | bytes 65683456 | tf_op jit(solution)/shard_map/reduce_sum | solution.py:40
  143.6 12.1 psum.36
  155.7 0.0 copy-start.13
  155.7 0.0 copy-done.5
  155.7 0.0 copy-done.7
  155.8 0.0 copy-done.9
  155.8 0.0 copy-done.11
  155.8 0.0 copy-done.15
  155.8 0.5 copy-done.13
  156.3 85.0 %fusion.2 = f32[1024,2048]{1,0:T(8,128)} fusion(bf16[16032,2048]{1,0:T(8,128)(2,1)} %param.13, f32[1024,16032]{0,1:T(8,128)} %get-tuple-element.17, f32[1024]{0:T(1024)S(1)} %get-tuple-element.11, f32[1024]{0:T(1024)S(1)} %get-tuple-element.10, s32[1024]{0:T(1024)S(1)} %bitcast.54), kind=kOutput, calls=%fused_computation.28 | convolution fusion | flops 67341582336 | bytes 139735040 | tf_op jit(solution)/shard_map/dot_general | solution.py:47
  241.3 0.0 all-reduce.4.cloned.1.call-update
  241.3 0.3 reduce-scatter.4.cloned.1.call-start
  241.6 83.5 %fusion.1 = f32[16032,2048]{1,0:T(8,128)} fusion(bf16[1024,2048]{1,0:T(8,128)(2,1)} %copy-done, f32[1024,16032]{0,1:T(8,128)} %get-tuple-element.17, f32[1024]{0:T(1024)S(1)} %get-tuple-element.11, f32[1024]{0:T(1024)S(1)} %get-tuple-element.10, s32[1024]{0:T(1024)S(1)} %bitcast.55), kind=kOutput, calls=%fused_computation.27 | convolution fusion | flops 67341582336 | bytes 201207808 | tf_op jit(solution)/shard_map/dot_general | solution.py:48
  325.1 0.0 copy-start.6
  325.1 0.0 copy-start.12
  325.2 0.0 copy-start.14
  325.2 0.0 copy-start.16
  325.2 0.0 copy-start.2
  325.2 0.0 copy-start.4
  325.2 0.0 reduce-scatter.4.cloned.1.call-update
  325.2 0.6 copy-done.6
  325.8 0.0 copy-done.8
  325.8 0.0 copy-done.10
  325.8 0.0 copy-done.12
  325.8 0.0 copy-done.14
  325.8 0.0 copy-done.16
  325.8 0.6 multiply_reduce_fusion.3
  326.5 32.7 %all-reduce.4.cloned.1.call-done = f32[1024,2048]{1,0:T(8,128)} async-done(((f32[1024,2048]{1,0:T(8,128)}), f32[1024,2048]{1,0:T(8,128)}) %all-reduce.4.cloned.1.call-update) | async-done | bytes 8388624 | tf_op jit(solution)/shard_map/psum | solution.py:47
  359.2 0.0 copy-done.2
  359.2 0.0 copy-done.4
  359.2 5.8 multiply_reduce_fusion
  365.0 6.0 all-reduce.1
  371.1 6.9 multiply_convert_fusion.1
  378.0 1361.8 %reduce-scatter.4.cloned.1.call-done = f32[8016,2048]{1,0:T(8,128)} async-done(((f32[16032,2048]{1,0:T(8,128)}), f32[8016,2048]{1,0:T(8,128)}) %reduce-scatter.4.cloned.1.call-update) | async-done | bytes 65667088
  (9 shorter events, 0.1 us)
Async XLA Ops:
  8.0 351.2 %all-reduce.4.cloned.1.call-start = ((), (), s32[]{:S(2)}) async-start(), calls=%async_computation.1 | async-start | bytes 16777216 | tf_op jit(solution)/shard_map/psum | solution.py:47
  25.4 1.9 copy-start.3
  26.1 1.2 copy-start.1
  30.5 78.6 %copy-start = (bf16[1024,2048]{1,0:T(8,128)(2,1)}, bf16[1024,2048]{1,0:T(8,128)(2,1)S(1)}, u32[]{:S(2)}) copy-start(bf16[1024,2048]{1,0:T(8,128)(2,1)S(1)} %multiply_convert_fusion.2) | copy-start | bytes 12582916
  122.2 33.5 %copy-start.5 = (f32[1,4,2,128]{3,1,2,0:T(4,128)S(1)}, f32[1,4,2,128]{3,1,2,0:T(4,128)}, u32[]{:S(2)}) copy-start(f32[1,4,2,128]{3,1,2,0:T(4,128)} %copy.11) | copy-start | bytes 12292
  122.2 33.5 %copy-start.7 = (f32[1,4,2,128]{3,1,2,0:T(4,128)S(1)}, f32[1,4,2,128]{3,1,2,0:T(4,128)}, u32[]{:S(2)}) copy-start(f32[1,4,2,128]{3,1,2,0:T(4,128)} %copy.15) | copy-start | bytes 12292
  122.3 33.5 %copy-start.9 = (f32[1,4,2,128]{3,1,2,0:T(4,128)S(1)}, f32[1,4,2,128]{3,1,2,0:T(4,128)}, u32[]{:S(2)}) copy-start(f32[1,4,2,128]{3,1,2,0:T(4,128)} %copy.12) | copy-start | bytes 12292
  122.3 33.5 %copy-start.11 = (f32[1,4,2,128]{3,1,2,0:T(4,128)S(1)}, f32[1,4,2,128]{3,1,2,0:T(4,128)}, u32[]{:S(2)}) copy-start(f32[1,4,2,128]{3,1,2,0:T(4,128)} %copy.16) | copy-start | bytes 12292
  122.3 33.5 %copy-start.15 = (pred[1024]{0:T(1024)(128)(4,1)S(1)}, pred[1024]{0:T(1024)(128)(4,1)}, u32[]{:S(2)}) copy-start(pred[1024]{0:T(1024)(128)(4,1)} %lt.13) | copy-start | bytes 3076
  155.7 0.6 copy-start.13
  241.3 1498.5 %reduce-scatter.4.cloned.1.call-start = ((), (), s32[]{:S(2)}) async-start(), calls=%async_computation.2 | async-start | bytes 197001216
  325.1 0.7 copy-start.6
  325.1 0.7 copy-start.8
  325.1 0.7 copy-start.10
  325.1 0.7 copy-start.12
  325.2 0.7 copy-start.14
  325.2 0.7 copy-start.16
  325.2 34.0 %copy-start.2 = (f32[2048]{0:T(1024)S(1)}, f32[2048]{0:T(1024)}, u32[]{:S(2)}) copy-start(f32[2048]{0:T(1024)} %copy-done.1) | copy-start | bytes 24580
  325.2 34.0 %copy-start.4 = (f32[1,4,2,128]{3,1,2,0:T(4,128)S(1)}, f32[1,4,2,128]{3,1,2,0:T(4,128)}, u32[]{:S(2)}) copy-start(f32[1,4,2,128]{3,1,2,0:T(4,128)} %copy-done.3) | copy-start | bytes 12292
Sparse Core Ops, SparseCore 0:
  241.5 117.6 all-reduce.3
Sparse Core Ops, SparseCore 1:
  325.3 1414.4 reduce-scatter.3
where the time goes:
time: 1750 us
  waiting for transfers between devices  1390 us (79%)
  matrix products  247 us (14%)
  other arithmetic  46.6 us (3%)
  blocking collectives  38.1 us (2%)
    unnamed x3, waiting for transfers between devices  1360 us
    dot_general x1, matrix products, local_step(): jnp.dot(d_logits, w_shard, preferred_element_type=jnp.float32)  85 us
    dot_general x1, matrix products, local_step(): lax.dot_general(d_logits, x_act, (((0,), (0,)), ((), ())), preferred_elem...  83.5 us
    dot_general x1, matrix products, local_step(): lax.dot_general(x_act, w_shard, (((1,), (1,)), ((), ())), preferred_eleme...  78.6 us
  transfers between devices with their start and end apart: 2, of which 2 were waited for; matrix products, arithmetic and copies ran while one was open for 6% of the time, Pallas kernels for 0%

commit v1 on v0

v1 whole, which is shorter than its diff:
```python
import jax
import jax.numpy as jnp
from jax import lax
from jax.sharding import PartitionSpec as P

EPSILON = 1e-5
CLIP_LOW = 0.8
CLIP_HIGH = 1.2
DUAL_CLIP = 3.0


def ppo_terms(logp, old_logp, advantages, tok_weight):
    prob_ratio = jnp.exp(logp - old_logp)
    loss_plain = -advantages * prob_ratio
    loss_clip = -advantages * jnp.clip(prob_ratio, CLIP_LOW, CLIP_HIGH)
    loss_max = jnp.maximum(loss_plain, loss_clip)
    dual_on = (advantages < 0) & (loss_max >= -DUAL_CLIP * advantages)
    tok_loss = jnp.where(dual_on, -DUAL_CLIP * advantages, loss_max)
    d_ratio = jnp.where(loss_plain >= loss_clip, -advantages, 0.0)
    d_ratio = jnp.where(dual_on, 0.0, d_ratio)
    return jnp.sum(tok_weight * tok_loss), tok_weight * d_ratio * prob_ratio


def norm_rows(h_float, gain_float):
    inv_rms = lax.rsqrt(jnp.mean(h_float * h_float, axis=-1, keepdims=True) + EPSILON)
    unit_rows = h_float * inv_rms
    return inv_rms, unit_rows, (unit_rows * gain_float).astype(jnp.bfloat16)


def solution(mesh):
    n_dp, n_tp = mesh.shape['dp'], mesh.shape['tp']

    def local_step(hidden, targets, resp_mask, old_logp, advantages, gain, w_shard):
        row_count, seq_len, width = hidden.shape
        v_dev = w_shard.shape[0] // n_dp
        n_tok = row_count * seq_len
        n_all = n_tok * n_dp
        piece = n_tok // n_tp
        dp_i, tp_i = lax.axis_index('dp'), lax.axis_index('tp')
        gain_float = gain.astype(jnp.float32)
        h_flat = hidden.reshape(n_tok, width)

        h_piece = lax.dynamic_slice_in_dim(h_flat, tp_i * piece, piece, 0).astype(jnp.float32)
        h_all = lax.all_gather(h_piece, ('dp', 'tp'), axis=0, tiled=True)
        small = jnp.stack([targets.reshape(n_tok).astype(jnp.float32), resp_mask.reshape(n_tok).astype(jnp.float32),
                           old_logp.reshape(n_tok), advantages.reshape(n_tok)])
        tok_info = lax.all_gather(small, 'dp', axis=1, tiled=True)
        tgt_all = tok_info[0].astype(jnp.int32)
        mask_all, old_all, adv_all = tok_info[1], tok_info[2], tok_info[3]
        row_sums = jnp.sum(mask_all.reshape(n_dp * row_count, seq_len), axis=1)
        rows_used = jnp.sum((row_sums > 0).astype(jnp.float32))
        tok_weight = (mask_all.reshape(n_dp * row_count, seq_len) / jnp.maximum(row_sums, 1.0)[:, None] / rows_used).reshape(n_all)

        x_all = norm_rows(h_all, gain_float)[2]
        w_half = lax.dynamic_slice_in_dim(w_shard, dp_i * v_dev, v_dev, 0)
        v_base = tp_i * (v_dev * n_dp) + dp_i * v_dev
        logits = lax.dot_general(w_half, x_all, (((1,), (1,)), ((), ())), preferred_element_type=jnp.float32)
        loc_max = jnp.max(logits, axis=0)
        is_target = lax.broadcasted_iota(jnp.int32, (v_dev, 1), 0) == (tgt_all - v_base)[None, :]
        loc_sum = jnp.sum(jnp.exp(logits - loc_max[None, :]), axis=0)
        loc_tgt = jnp.sum(jnp.where(is_target, logits, 0.0), axis=0)
        stats = lax.all_gather(jnp.stack([loc_max, loc_sum, loc_tgt]), ('dp', 'tp'), axis=0, tiled=False)
        row_max = jnp.max(stats[:, 0], axis=0)
        log_norm = row_max + jnp.log(jnp.sum(stats[:, 1] * jnp.exp(stats[:, 0] - row_max[None]), axis=0))
        logp = jnp.sum(stats[:, 2], axis=0) - log_norm
        total_loss, d_logp = ppo_terms(logp, old_all, adv_all, tok_weight)

        soft_probs = jnp.exp(logits - log_norm[None, :])
        d_logits = (d_logp[None, :] * (jnp.where(is_target, 1.0, 0.0) - soft_probs)).astype(jnp.bfloat16)
        dx_part = lax.dot_general(d_logits, w_half, (((0,), (0,)), ((), ())), preferred_element_type=jnp.float32)
        dx_mine = lax.psum_scatter(dx_part, ('dp', 'tp'), scatter_dimension=0, tiled=True)
        d_head = lax.dot_general(d_logits, x_all, (((1,), (0,)), ((), ())), preferred_element_type=jnp.float32)
        inv_rms, unit_rows, _ = norm_rows(h_piece, gain_float)
        d_gain = lax.psum(jnp.sum(dx_mine * unit_rows, axis=0), ('dp', 'tp'))
        d_unit = dx_mine * gain_float
        dh_piece = inv_rms * (d_unit - unit_rows * jnp.mean(d_unit * unit_rows, axis=-1, keepdims=True))
        dh = lax.all_gather(dh_piece, 'tp', axis=0, tiled=True)
        d_hidden = (dh + 0.0 * gain_float).astype(jnp.bfloat16)
        return total_loss, d_hidden.reshape(row_count, seq_len, width), d_head, d_gain

    row_spec = P('dp', None)
    return jax.shard_map(local_step, mesh=mesh, in_specs=(P('dp', None, None), row_spec, row_spec, row_spec, row_spec, P(None), P('tp', None)), out_specs=(P(), P('dp', None, None), P(('tp', 'dp'), None), P(None)), check_vma=False)
```

time: 1750 us -> 613 us (0.35)
  waiting for transfers between devices: 1390 us -> 242 us
    unnamed x3, waiting for transfers between devices: 1360 us -> 0.05 us
    reduce_scatter x0 -> x1, waiting for transfers between devices: none -> 175 us  [local_step(): lax.psum_scatter(dx_part, ('dp', 'tp'), scatter_dimension=0, tiled=True)]
    all_gather x0 -> x2, waiting for transfers between devices: none -> 67.2 us  [the longest x1 67.2 us: local_step(): h_all = lax.all_gather(h_piece, ('dp', 'tp'), axis=0, tiled=True)]
    psum x1 -> x0, waiting for transfers between devices: 32.7 us -> none  [local_step(): lax.psum(jnp.dot(d_logits, w_shard, preferred_element_type=jnp.float32),...]
    all_gather x0 -> x2, blocking collectives: none -> 19.5 us  [the longest x1 13.8 us: local_step(): lax.all_gather(jnp.stack([loc_max, loc_sum, loc_tgt]), ('dp', 'tp'), axis...]
  transfers between devices with their start and end apart: 2 -> 3, of which waited for: 2 -> 2; matrix products, arithmetic and copies ran while one was open for 6% -> 16% of each run, Pallas kernels for 0% -> 0%
where the time goes in v1:
time: 613 us; the launch traced here: 612 us
  matrix products  253 us (41%)
  waiting for transfers between devices  242 us (39%)
  blocking collectives  50.4 us (8%)
  other arithmetic  49.7 us (8%)
  between operations  13.9 us (2%)
    reduce_scatter x1, waiting for transfers between devices, local_step(): lax.psum_scatter(dx_part, ('dp', 'tp'), scatter_dimension=0, tiled=True)  175 us
    dot_general x1, matrix products, local_step(): lax.dot_general(d_logits, w_half, (((0,), (0,)), ((), ())), preferred_ele...  86.3 us
    dot_general x1, matrix products, local_step(): lax.dot_general(d_logits, x_all, (((1,), (0,)), ((), ())), preferred_elem...  85.8 us
    dot_general x1, matrix products, local_step(): lax.dot_general(w_half, x_all, (((1,), (1,)), ((), ())), preferred_elemen...  80.8 us
    all_gather x1, waiting for transfers between devices, local_step(): h_all = lax.all_gather(h_piece, ('dp', 'tp'), axis=0, tiled=True)  67.2 us
    psum x1, blocking collectives, local_step(): d_gain = lax.psum(jnp.sum(dx_mine * unit_rows, axis=0), ('dp', 'tp'))  30.9 us
    reduce_sum x1, other arithmetic, local_step(): loc_sum = jnp.sum(jnp.exp(logits - loc_max[None, :]), axis=0)  21.3 us
    all_gather x1, blocking collectives, local_step(): lax.all_gather(jnp.stack([loc_max, loc_sum, loc_tgt]), ('dp', 'tp'), axis...  13.8 us
  transfers between devices with their start and end apart: 3, of which 2 were waited for; matrix products, arithmetic and copies ran while one was open for 16% of the time, Pallas kernels for 0%

profile of v1, /device:TPU:0, one launch (start us, length us, event | category | flops | bytes accessed | tf_op | source)
XLA Modules:
  0.0 612.4 jit_solution(7638673469245520280)
XLA Ops:
  7.2 0.0 all-gather.5.cloned.1.call-start
  7.2 2.1 dynamic-slice_convert_fusion
  9.3 0.0 all-gather.5.cloned.1.call-update
  9.4 0.0 reduce-scatter.2.cloned.1.call-start
  9.4 0.7 convert_element_type.54
  10.1 0.7 convert_bitcast_fusion.1
  10.8 0.7 convert_bitcast_fusion
  11.5 0.7 copy.17
  12.2 0.7 copy.18
  12.9 5.7 all_gather.15
  18.6 0.0 copy-start
  18.6 0.6 fusion.12
  19.2 0.1 reduce_sum.99
  19.4 0.6 fusion.8
  20.0 0.6 maximum_multiply_fusion
  20.6 0.1 broadcast_bitcast_fusion
  20.7 0.6 copy.19
  21.3 0.6 copy.20
  21.9 0.6 compare_reduce_fusion
  22.5 67.2 %all-gather.5.cloned.1.call-done = f32[2048,2048]{1,0:T(8,128)} async-done(((f32[128,2048]{1,0:T(8,128)}), f32[2048,2048]{1,0:T(8,128)}) %all-gather.5.cloned.1.call-update) | async-done | bytes 16777232 | tf_op jit(solution)/shard_map/all_gather | solution.py:44
  89.7 6.9 %multiply_reduce_fusion = f32[2048]{0:T(1024)S(1)} fusion(f32[2048,2048]{1,0:T(8,128)} %all-gather.5.cloned.1.call-done), kind=kLoop, calls=%fused_computation.9 | loop fusion | flops 8386560 | bytes 16785408 | tf_op jit(solution)/shard_map/reduce_sum | solution.py:25
  96.7 80.8 %fusion.13 = (f32[2048]{0:T(1024)S(1)}, f32[8016,2048]{1,0:T(8,128)}) fusion(f32[2048,2048]{1,0:T(8,128)} %all-gather.5.cloned.1.call-done, f32[2048]{0:T(1024)S(1)} %convert_element_type.54, f32[2048]{0:T(1024)S(1)} %add_rsqrt_fusion, bf16[16032,2048]{1,0:T(8,128)(2,1)} %param.13, s32[]{:T(128)S(6)} %select_n.28), kind=kOutput, calls=%fused_computation.52 | convolution fusion | flops 67272081408 | bytes 115302400 | tf_op jit(solution)/shard_map/dot_general | solution.py:57
  177.5 0.0 copy-done
  177.5 0.0 copy-start.4
  177.5 0.0 copy-start.5
  177.5 0.0 copy-start.6
  177.5 0.0 copy-start.7
  177.5 0.0 copy-start.8
  177.5 0.0 copy-start.11
  177.5 0.0 copy-start.3
  177.6 0.0 copy-start.1
  177.6 21.3 %exponential_reduce_fusion = (f32[2048]{0:T(1024)S(1)}, f32[2048]{0:T(1024)S(1)}) fusion(f32[8016,2048]{1,0:T(8,128)} %get-tuple-element.23, f32[2048]{0:T(1024)S(1)} %get-tuple-element.22, s32[2048]{0:T(1024)S(1)} %bitcast.55), kind=kLoop, calls=%fused_computation.3 | loop fusion | flops 82079744 | bytes 65699840 | tf_op jit(solution)/shard_map/reduce_sum | solution.py:60
  198.9 13.8 %all-gather.1 = f32[16,3,2048]{2,1,0:T(4,128)S(1)} all-gather(f32[1,3,2048]{2,1,0:T(4,128)S(1)} %maximum_bitcast_fusion), channel_id=2, replica_groups=mesh['dp'=2,'tp'=8] {'dp','tp'}, dimensions={0}, use_global_device_ids=true | all-gather | bytes 417792 | tf_op jit(solution)/shard_map/all_gather | solution.py:62
  212.8 0.3 slice_reduce_fusion.2
  213.1 0.1 fusion.5
  213.2 0.0 copy-done.4
  213.3 0.0 copy-done.5
  213.3 0.0 copy-done.6
  213.3 0.0 copy-done.7
  213.3 0.0 copy-done.8
  213.3 0.0 copy-done.11
  213.3 0.6 multiply_reduce_fusion.4
  213.9 0.0 copy-done.3
  213.9 0.0 copy-done.1
  213.9 0.1 multiply_multiply_fusion
  214.0 0.0 copy-start.10
  214.0 86.3 %fusion = f32[2048,2048]{1,0:T(8,128)} fusion(bf16[16032,2048]{1,0:T(8,128)(2,1)} %param.13, s32[]{:T(128)S(6)} %select_n.28, f32[8016,2048]{1,0:T(8,128)} %get-tuple-element.23, f32[2048]{0:T(1024)S(1)} %get-tuple-element.12, f32[2048]{0:T(1024)S(1)} %bitcast.69, s32[2048]{0:T(1024)S(1)} %bitcast.56), kind=kOutput, calls=%fused_computation.4 | convolution fusion | flops 67341582336 | bytes 115302400 | tf_op jit(solution)/shard_map/dot_general | solution.py:70
  300.4 0.0 reduce-scatter.2.cloned.1.call-update
  300.4 0.3 all-gather.7.cloned.1.call-start
  300.7 1.2 multiply_reduce_fusion.3
  301.9 175.0 %reduce-scatter.2.cloned.1.call-done = f32[128,2048]{1,0:T(8,128)} async-done(((f32[2048,2048]{1,0:T(8,128)}), f32[128,2048]{1,0:T(8,128)}) %reduce-scatter.2.cloned.1.call-update) | async-done | bytes 1048592 | tf_op jit(solution)/shard_map/reduce_scatter | solution.py:71
  477.0 2.3 multiply_reduce_fusion.1
  479.3 2.7 subtract_multiply_fusion
  482.0 0.0 all-gather.7.cloned.1.call-update
  482.0 0.0 copy-done.10
  482.0 0.6 broadcast_multiply_fusion
  482.6 0.0 copy-start.2
  482.6 0.0 copy-start.9
  482.6 85.8 %fusion.11 = f32[8016,2048]{1,0:T(8,128)} fusion(f32[2048,2048]{1,0:T(8,128)} %all-gather.5.cloned.1.call-done, f32[2048]{0:T(1024)S(1)} %convert_element_type.54, f32[2048]{0:T(1024)S(1)} %add_rsqrt_fusion, f32[8016,2048]{1,0:T(8,128)} %get-tuple-element.23, f32[2048]{0:T(1024)S(1)} %get-tuple-element.12, f32[2048]{0:T(1024)S(1)} %bitcast.70, ...), kind=kOutput, calls=%fused_computation.50 | convolution fusion | flops 67354165248 | bytes 148152320 | tf_op jit(solution)/shard_map/dot_general | solution.py:72
  568.4 0.0 copy-done.2
  568.4 30.9 %psum.7 = f32[2048]{0:T(1024)} all-reduce(f32[2048]{0:T(1024)S(1)} %copy-done.2), channel_id=1, replica_groups=mesh['dp'=2,'tp'=8] {'dp','tp'}, use_global_device_ids=true, to_apply=%region_14.15 | all-reduce | flops 2048 | bytes 16384 | tf_op jit(solution)/shard_map/psum | solution.py:74
  599.3 0.0 all-gather.7.cloned.1.call-done
  599.3 0.0 copy-done.9
  599.3 6.6 %add_convert_fusion = bf16[1024,2048]{1,0:T(8,128)(2,1)} fusion(f32[1024,2048]{1,0:T(8,128)} %all-gather.7.cloned.1.call-done, f32[2048]{0:T(1024)S(1)} %copy-done.9), kind=kLoop, calls=%fused_computation.10 | loop fusion | flops 4194304 | bytes 12591104 | tf_op jit(solution)/shard_map/convert_element_type | solution.py:78
  (9 shorter events, 0.1 us)
Async XLA Ops:
  7.2 82.5 %all-gather.5.cloned.1.call-start = ((), (), s32[]{:S(2)}) async-start(), calls=%async_computation.1 | async-start | bytes 17825792 | tf_op jit(solution)/shard_map/all_gather | solution.py:44
  9.4 467.6 %reduce-scatter.2.cloned.1.call-start = ((), (), s32[]{:S(2)}) async-start(), calls=%async_computation.2 | async-start | bytes 17825792 | tf_op jit(solution)/shard_map/reduce_scatter | solution.py:71
  18.6 158.9 %copy-start = (f32[4,2048]{1,0:T(4,128)}, f32[4,2048]{1,0:T(4,128)S(1)}, u32[]{:S(2)}) copy-start(f32[4,2048]{1,0:T(4,128)S(1)} %all_gather.15) | copy-start | bytes 98308
  177.5 35.8 %copy-start.4 = (f32[1,4,4,128]{3,1,2,0:T(4,128)S(1)}, f32[1,4,4,128]{3,1,2,0:T(4,128)}, u32[]{:S(2)}) copy-start(f32[1,4,4,128]{3,1,2,0:T(4,128)} %copy.19) | copy-start | bytes 24580
  177.5 35.8 %copy-start.5 = (f32[1,2048]{1,0:T(1,128)S(1)}, f32[1,2048]{1,0:T(1,128)}, u32[]{:S(2)}) copy-start(f32[1,2048]{1,0:T(1,128)} %get-tuple-element.15) | copy-start | bytes 24580
  177.5 35.8 %copy-start.6 = (f32[1,2048]{1,0:T(1,128)S(1)}, f32[1,2048]{1,0:T(1,128)}, u32[]{:S(2)}) copy-start(f32[1,2048]{1,0:T(1,128)} %get-tuple-element.17) | copy-start | bytes 24580
  177.5 35.8 %copy-start.7 = (f32[1,2048]{1,0:T(1,128)S(1)}, f32[1,2048]{1,0:T(1,128)}, u32[]{:S(2)}) copy-start(f32[1,2048]{1,0:T(1,128)} %get-tuple-element.18) | copy-start | bytes 24580
  177.5 35.8 %copy-start.8 = (f32[1,2048]{1,0:T(1,128)S(1)}, f32[1,2048]{1,0:T(1,128)}, u32[]{:S(2)}) copy-start(f32[1,2048]{1,0:T(1,128)} %get-tuple-element.19) | copy-start | bytes 24580
  177.5 35.8 %copy-start.11 = (pred[2048]{0:T(1024)(128)(4,1)S(1)}, pred[2048]{0:T(1024)(128)(4,1)}, u32[]{:S(2)}) copy-start(pred[2048]{0:T(1024)(128)(4,1)} %compare_reduce_fusion) | copy-start | bytes 6148
  177.5 36.4 %copy-start.3 = (f32[1,1,4,512]{3,1,2,0:T(1,128)S(1)}, f32[1,1,4,512]{3,1,2,0:T(1,128)}, u32[]{:S(2)}) copy-start(f32[1,1,4,512]{3,1,2,0:T(1,128)} %copy.20) | copy-start | bytes 24580
  177.6 36.4 %copy-start.1 = (f32[4,2048]{1,0:T(4,128)S(1)}, f32[4,2048]{1,0:T(4,128)}, u32[]{:S(2)}) copy-start(f32[4,2048]{1,0:T(4,128)} %copy-done) | copy-start | bytes 98308
  214.0 268.0 %copy-start.10 = (bf16[2048]{0:T(1024)(128)(2,1)S(1)}, bf16[2048]{0:T(1024)(128)(2,1)}, u32[]{:S(2)}) copy-start(bf16[2048]{0:T(1024)(128)(2,1)} %param.12) | copy-start | bytes 12292
  300.4 298.9 %all-gather.7.cloned.1.call-start = ((), (), s32[]{:S(2)}) async-start(), calls=%async_computation.3 | async-start | bytes 9437184 | tf_op jit(solution)/shard_map/all_gather | solution.py:77
  482.6 85.9 %copy-start.2 = (f32[2048]{0:T(1024)S(1)}, f32[2048]{0:T(1024)}, u32[]{:S(2)}) copy-start(f32[2048]{0:T(1024)} %get-tuple-element.6) | copy-start | bytes 24580
  482.6 116.7 %copy-start.9 = (f32[2048]{0:T(1024)S(1)}, f32[2048]{0:T(1024)}, u32[]{:S(2)}) copy-start(f32[2048]{0:T(1024)} %broadcast_multiply_fusion) | copy-start | bytes 24580
Sparse Core Ops, SparseCore 0:
  10.8 78.8 all-gather.4
  300.5 176.3 reduce-scatter.1
  482.1 48.3 all-gather.6

commit v2 on v1

v2 whole, which is shorter than its diff:
```python
import functools

import jax
import jax.numpy as jnp
from jax import lax
from jax.experimental import pallas as pl
from jax.experimental.pallas import tpu as pltpu
from jax.sharding import PartitionSpec as P

EPSILON = 1e-5
CLIP_LOW = 0.8
CLIP_HIGH = 1.2
DUAL_CLIP = 3.0
MESH = pl.DeviceIdType.MESH
F32, BF16 = jnp.float32, jnp.bfloat16
VMEM_MAX = 67043328
N_CHUNK = 4
V_BLK = 2672
PART_COLS = ((0, 768), (768, 640), (1408, 640))


def ppo_terms(logp, old_logp, advantages, tok_weight):
    prob_ratio = jnp.exp(logp - old_logp)
    loss_plain = -advantages * prob_ratio
    loss_clip = -advantages * jnp.clip(prob_ratio, CLIP_LOW, CLIP_HIGH)
    loss_max = jnp.maximum(loss_plain, loss_clip)
    dual_on = (advantages < 0) & (loss_max >= -DUAL_CLIP * advantages)
    tok_loss = jnp.where(dual_on, -DUAL_CLIP * advantages, loss_max)
    d_ratio = jnp.where(loss_plain >= loss_clip, -advantages, 0.0)
    d_ratio = jnp.where(dual_on, 0.0, d_ratio)
    return jnp.sum(tok_weight * tok_loss), tok_weight * d_ratio * prob_ratio


def norm_rows(h_float, gain_float):
    inv_rms = lax.rsqrt(jnp.mean(h_float * h_float, axis=-1, keepdims=True) + EPSILON)
    unit_rows = h_float * inv_rms
    return inv_rms, unit_rows, (unit_rows * gain_float).astype(BF16)


def logits_kernel(tb, sub, dp_ref, x_ref, w_ref, tgt_ref, z_ref, m_ref, s_ref, t_ref):
    v, t = pl.program_id(0), pl.program_id(1)
    rows = w_ref.shape[0]
    for j in range(tb // sub):
        jc = pl.ds(pl.multiple_of(t * tb + j * sub, sub), sub)
        z = lax.dot_general(w_ref[...], x_ref[j * sub:(j + 1) * sub, :], (((1,), (1,)), ((), ())), preferred_element_type=F32)
        z_ref[:, j * sub:(j + 1) * sub] = z
        z3 = z.reshape(rows // 8, 8, sub)
        m_old = jnp.where(v == 0, -3e38, m_ref[:, jc])
        s_old = jnp.where(v == 0, 0.0, s_ref[:, jc])
        t_old = jnp.where(v == 0, 0.0, t_ref[:, jc])
        m_new = jnp.maximum(m_old, jnp.max(z3, axis=0))
        s_ref[:, jc] = s_old * jnp.exp(m_old - m_new) + jnp.sum(jnp.exp(z3 - m_new[None]), axis=0)
        m_ref[:, jc] = m_new
        hit = lax.broadcasted_iota(jnp.int32, (rows, sub), 0) == tgt_ref[0:1, jc] - v * rows
        t_ref[:, jc] = t_old + jnp.sum(jnp.where(hit, z, 0.0).reshape(rows // 8, 8, sub), axis=0)


def token_logits(x_rows, w_shard, tgt_rel, dp_i, v_dev):
    n_tok, width = x_rows.shape
    tb, n_v = 512, v_dev // V_BLK
    full = pl.BlockSpec((8, n_tok), lambda v, t, d: (0, 0))
    z_t, m, s, zt = pl.pallas_call(
        functools.partial(logits_kernel, tb, 256),
        grid_spec=pltpu.PrefetchScalarGridSpec(
            num_scalar_prefetch=1, grid=(n_v, n_tok // tb),
            in_specs=[pl.BlockSpec((tb, width), lambda v, t, d: (t, 0)),
                      pl.BlockSpec((V_BLK, width), lambda v, t, d: (d[0] * n_v + v, 0)),
                      pl.BlockSpec((1, n_tok), lambda v, t, d: (0, 0))],
            out_specs=[pl.BlockSpec((V_BLK, tb), lambda v, t, d: (v, t)), full, full, full]),
        out_shape=[jax.ShapeDtypeStruct((v_dev, n_tok), F32)] + [jax.ShapeDtypeStruct((8, n_tok), F32)] * 3,
        compiler_params=pltpu.CompilerParams(vmem_limit_bytes=VMEM_MAX),
        cost_estimate=pl.CostEstimate(flops=2 * v_dev * n_tok * width, bytes_accessed=v_dev * n_tok * 4 + v_dev * width * 2, transcendentals=v_dev * n_tok),
    )(dp_i.reshape(1), x_rows, w_shard, tgt_rel)
    m_loc = jnp.max(m, axis=0)
    lse_loc = m_loc + jnp.log(jnp.sum(s * jnp.exp(m - m_loc[None]), axis=0))
    return z_t, lse_loc, jnp.sum(zt, axis=0)


def dx_kernel(v_dev, zo_ref, zr_ref, lse_ref, dl_ref, tgt_ref, w_ref, hp_ref, g_ref, dz_ref, out_ref,
              acc, got0, got1a, got1b, got1c, got2a, got2b, got2c, got3a, got3b, got3c,
              s2a, s2b, s2c, s3a, s3b, s3c, dg, dg_got, snd0, rcv0, snd, rcv, snd_g, rcv_g):
    k, v = pl.program_id(0), pl.program_id(1)
    dp, tp = lax.axis_index('dp'), lax.axis_index('tp')
    core, xx, yy = tp % 2, (tp // 2) % 2, tp // 4
    by_core = (dp, yy * 4 + xx * 2 + (1 - core))
    by_x = (dp, yy * 4 + (1 - xx) * 2 + core)
    by_y = (dp, (1 - yy) * 4 + xx * 2 + core)
    by_z = (1 - dp, tp)
    got1, got2, got3 = (got1a, got1b, got1c), (got2a, got2b, got2c), (got3a, got3b, got3c)
    s2, s3 = (s2a, s2b, s2c), (s3a, s3b, s3c)
    cols = [pl.ds(a, n) for a, n in PART_COLS]
    peers = ((by_z, by_y, by_x), (by_y, by_x, by_z), (by_x, by_z, by_y))

    def copy0(j):
        p = j % 2
        return pltpu.make_async_remote_copy(acc.at[p, 1 - core], got0.at[p], snd0.at[p], rcv0.at[p], device_id=by_core, device_id_type=MESH)

    def copy1(j, part):
        p = j % 2
        src = (acc.at[p, core, 1, :, :, :, cols[0]], acc.at[p, core, :, 1 - yy, :, :, cols[1]], acc.at[p, core, :, :, 1 - xx, :, cols[2]])[part]
        return pltpu.make_async_remote_copy(src, got1[part].at[p], snd.at[0, part, p], rcv.at[0, part, p], device_id=peers[part][0], device_id_type=MESH)

    def copy2(j, part):
        p = j % 2
        src = (s2a.at[1 - yy], s2b.at[:, 1 - xx], s2c.at[1])[part]
        return pltpu.make_async_remote_copy(src, got2[part].at[p], snd.at[1, part, p], rcv.at[1, part, p], device_id=peers[part][1], device_id_type=MESH)

    def copy3(j, part):
        p = j % 2
        src = (s3a.at[1 - xx], s3b.at[1], s3c.at[1 - yy])[part]
        return pltpu.make_async_remote_copy(src, got3[part].at[p], snd.at[2, part, p], rcv.at[2, part, p], device_id=peers[part][2], device_id_type=MESH)

    def stage_a(j):
        copy0(j).wait()
        p = j % 2
        acc[p, core] = acc[p, core] + got0[p]
        for part in range(3):
            copy1(j, part).start()

    def stage_b(j):
        p = j % 2
        for part in range(3):
            copy1(j, part).wait()
        s2a[...] = acc[p, core, 0, :, :, :, cols[0]] + got1a[p]
        s2b[...] = acc[p, core, :, yy, :, :, cols[1]] + got1b[p]
        s2c[...] = acc[p, core, :, :, xx, :, cols[2]] + got1c[p]
        for part in range(3):
            copy2(j, part).start()

    def stage_c(j):
        p = j % 2
        for part in range(3):
            copy2(j, part).wait()
        s3a[...] = s2a[yy] + got2a[p]
        s3b[...] = s2b[:, xx] + got2b[p]
        s3c[...] = s2c[0] + got2c[p]
        for part in range(3):
            copy3(j, part).start()

    def stage_d(j):
        p = j % 2
        for part in range(3):
            copy3(j, part).wait()
        d_act = jnp.concatenate([s3a[xx] + got3a[p], s3b[0] + got3b[p], s3c[yy] + got3c[p]], axis=1)
        rows = pl.ds(pl.multiple_of(j * 32, 32), 32)
        h_rows = hp_ref[rows, :]
        inv_rms = lax.rsqrt(jnp.mean(h_rows * h_rows, axis=-1, keepdims=True) + EPSILON)
        unit_rows = h_rows * inv_rms
        dg[...] += jnp.sum((d_act * unit_rows).reshape(4, 8, d_act.shape[1]), axis=0)
        d_unit = d_act * g_ref[...]
        out_ref[rows, :] = d_unit - unit_rows * jnp.mean(d_unit * unit_rows, axis=-1, keepdims=True)

    @pl.when((k == 0) & (v == 0))
    def _():
        barrier = pltpu.get_barrier_semaphore()
        for peer in (by_core, by_x, by_y, by_z):
            pl.semaphore_signal(barrier, inc=1, device_id=peer, device_id_type=MESH)
        pl.semaphore_wait(barrier, 4)
        dg[...] = jnp.zeros_like(dg)

    @pl.when((k >= 2) & (v == 0))
    def _():
        stage_c(k - 2)

    @pl.when((k >= 1) & (v == 1))
    def _():
        stage_a(k - 1)

    @pl.when((k >= 2) & (v == 1))
    def _():
        stage_d(k - 2)

    @pl.when((k >= 1) & (v == 2))
    def _():
        stage_b(k - 1)

    z = jnp.concatenate([zo_ref[:, 0:128], zr_ref[:, 0:128], zo_ref[:, 128:256], zr_ref[:, 128:256]], axis=1)
    soft = jnp.exp(z - lse_ref[...])
    first = (tp * 2 + dp) * v_dev + v * z.shape[0]
    hit = lax.broadcasted_iota(jnp.int32, z.shape, 0) == tgt_ref[...] - first
    dz = (dl_ref[...] * (jnp.where(hit, 1.0, 0.0) - soft)).astype(BF16)
    dz_ref[...] = dz
    half = w_ref.shape[1] // 2
    for side in range(2):
        c = pl.ds(side * half, half)
        part_dx = lax.dot_general(dz_ref[...], w_ref[:, c], (((0,), (0,)), ((), ())), preferred_element_type=F32)
        acc[k % 2, :, :, :, :, :, c] = jnp.where(v == 0, 0.0, acc[k % 2, :, :, :, :, :, c]) + part_dx.reshape(2, 2, 2, 2, 32, half)

    @pl.when(v == 2)
    def _():
        copy0(k).start()

    @pl.when((k == N_CHUNK - 1) & (v == 2))
    def _():
        stage_c(N_CHUNK - 2)
        stage_a(N_CHUNK - 1)
        stage_d(N_CHUNK - 2)
        stage_b(N_CHUNK - 1)
        stage_c(N_CHUNK - 1)
        stage_d(N_CHUNK - 1)
        last = pltpu.make_async_remote_copy(dg, dg_got, snd_g, rcv_g, device_id=by_z, device_id_type=MESH)
        last.start()
        last.wait()
        out_ref[pl.ds(128, 8), :] = dg[...] + dg_got[...]


def dx_reduced(z_own, z_other, lse, d_logp, tgt, w_shard, h_piece, gain_float, v_dev):
    width = w_shard.shape[1]
    n_all = lse.shape[1]
    tb = n_all // N_CHUNK
    row = pl.BlockSpec((1, tb), lambda k, v: (0, k))
    sizes = [n for _, n in PART_COLS]
    vm = lambda *shape: pltpu.VMEM(shape, F32)
    return pl.pallas_call(
        functools.partial(dx_kernel, v_dev),
        grid=(N_CHUNK, v_dev // V_BLK),
        in_specs=[pl.BlockSpec((V_BLK, tb // 2), lambda k, v: (v, k)), pl.BlockSpec((V_BLK, tb // 2), lambda k, v: (v, k)),
                  row, row, row,
                  pl.BlockSpec((V_BLK, width), lambda k, v: (lax.axis_index('dp') * (v_dev // V_BLK) + v, 0)),
                  pl.BlockSpec(h_piece.shape, lambda k, v: (0, 0), pipeline_mode=pl.Buffered(1)),
                  pl.BlockSpec((1, width), lambda k, v: (0, 0))],
        out_specs=[pl.BlockSpec((V_BLK, tb), lambda k, v: (v, k)), pl.BlockSpec((h_piece.shape[0] + 8, width), lambda k, v: (0, 0), pipeline_mode=pl.Buffered(1))],
        out_shape=[jax.ShapeDtypeStruct((v_dev, n_all), BF16), jax.ShapeDtypeStruct((h_piece.shape[0] + 8, width), F32)],
        scratch_shapes=[vm(2, 2, 2, 2, 2, 32, width), vm(2, 2, 2, 2, 32, width)]
        + [vm(2, 2, 2, 32, n) for n in sizes] + [vm(2, 2, 32, n) for n in sizes] + [vm(2, 32, n) for n in sizes]
        + [vm(2, 2, 32, n) for n in sizes] + [vm(2, 32, n) for n in sizes]
        + [vm(8, width), vm(8, width),
           pltpu.SemaphoreType.DMA((2,)), pltpu.SemaphoreType.DMA((2,)),
           pltpu.SemaphoreType.DMA((3, 3, 2)), pltpu.SemaphoreType.DMA((3, 3, 2)),
           pltpu.SemaphoreType.DMA, pltpu.SemaphoreType.DMA],
        compiler_params=pltpu.CompilerParams(collective_id=0, has_side_effects=True, vmem_limit_bytes=VMEM_MAX),
        cost_estimate=pl.CostEstimate(flops=2 * v_dev * n_all * width, bytes_accessed=v_dev * n_all * 6 + 4 * v_dev * width * 2, transcendentals=v_dev * n_all),
    )(z_own, z_other, lse, d_logp, tgt, w_shard, h_piece, gain_float)


def head_kernel(dz_ref, xo_ref, xr_ref, o_ref, x_all, sem):
    @pl.when(pl.program_id(0) == 0)
    def _():
        copies = [pltpu.make_async_copy(src.at[i], x_all.at[i, z], sem.at[i, z])
                  for i in range(x_all.shape[0]) for z, src in enumerate((xo_ref, xr_ref))]
        for copy in copies:
            copy.start()
        for copy in copies:
            copy.wait()

    o_ref[...] = jnp.dot(dz_ref[...], x_all[...].reshape(dz_ref.shape[1], o_ref.shape[1]), preferred_element_type=F32)


def head_grad(dz, x_own, x_other):
    v_dev, n_all = dz.shape
    width = x_own.shape[1]
    vb, groups = 512, n_all // 256
    return pl.pallas_call(
        head_kernel, grid=(pl.cdiv(v_dev, vb),),
        in_specs=[pl.BlockSpec((vb, n_all), lambda v: (v, 0)), pl.BlockSpec(memory_space=pl.ANY), pl.BlockSpec(memory_space=pl.ANY)],
        out_specs=pl.BlockSpec((vb, width), lambda v: (v, 0)),
        out_shape=jax.ShapeDtypeStruct((v_dev, width), F32),
        scratch_shapes=[pltpu.VMEM((groups, 2, 128, width), BF16), pltpu.SemaphoreType.DMA((groups, 2))],
        compiler_params=pltpu.CompilerParams(vmem_limit_bytes=VMEM_MAX),
        cost_estimate=pl.CostEstimate(flops=2 * v_dev * n_all * width, bytes_accessed=v_dev * width * 4 + v_dev * n_all * 2, transcendentals=0),
    )(dz, x_own.reshape(groups, 128, width), x_other.reshape(groups, 128, width))


def solution(mesh):
    n_dp, n_tp = mesh.shape['dp'], mesh.shape['tp']

    def local_step(hidden, targets, resp_mask, old_logp, advantages, gain, w_shard):
        row_count, seq_len, width = hidden.shape
        v_dev = w_shard.shape[0] // n_dp
        n_tok = row_count * seq_len
        n_all = n_tok * n_dp
        piece = n_tok // n_tp
        dp_i, tp_i = lax.axis_index('dp'), lax.axis_index('tp')
        gain_float = gain.astype(F32)
        h_flat = hidden.reshape(n_tok, width)

        seg = piece // N_CHUNK
        place = (tp_i % 2) * 4 + tp_i // 2
        h_piece = lax.dynamic_index_in_dim(h_flat.reshape(N_CHUNK, n_tp, seg, width), place, 1, keepdims=False).reshape(piece, width).astype(F32)
        h_all = lax.all_gather(h_piece, ('dp', 'tp'), axis=0, tiled=True)

        row_sums = jnp.sum(resp_mask, axis=1).astype(F32)
        used = jnp.sum((row_sums > 0).astype(F32))
        share = (resp_mask.astype(F32) / jnp.maximum(row_sums, 1.0)[:, None]).reshape(n_tok)
        small = jnp.stack([targets.reshape(n_tok).astype(F32), share, old_logp.reshape(n_tok),
                           advantages.reshape(n_tok), jnp.full((n_tok,), used)])
        info = lax.all_gather(small, 'dp', axis=0)
        tgt_abs = info[:, 0].astype(jnp.int32)

        def to_mine(a):
            b = a.reshape(n_dp, 2 * N_CHUNK, 128)
            return jnp.stack([jnp.where(dp_i == 0, b[0], b[1]), jnp.where(dp_i == 0, b[1], b[0])], axis=1).reshape(1, n_all)

        v_base = (tp_i * n_dp + dp_i) * v_dev
        tgt_own = lax.dynamic_index_in_dim(tgt_abs, dp_i, 0, keepdims=True) - v_base
        tgt_other = lax.dynamic_index_in_dim(tgt_abs, 1 - dp_i, 0, keepdims=True) - v_base

        inv_own, _, x_own = norm_rows(h_flat.astype(F32), gain_float)
        x_own = lax.optimization_barrier(x_own)
        z_own, lse_own, zt_own = token_logits(x_own, w_shard, tgt_own, dp_i, v_dev)
        h_all, lse_own, zt_own = lax.optimization_barrier((h_all, lse_own, zt_own))
        h_other = lax.dynamic_index_in_dim(h_all.reshape(n_dp, n_tp // 2, 2, N_CHUNK, seg, width), 1 - dp_i, 0, keepdims=False)
        x_other = norm_rows(h_other, gain_float)[2].transpose(2, 1, 0, 3, 4).reshape(n_tok, width)
        z_other, lse_other, zt_other = token_logits(x_other, w_shard, tgt_other, dp_i, v_dev)

        own_first = dp_i == 0
        mine = jnp.stack([jnp.stack([lse_own, zt_own]), jnp.stack([lse_other, zt_other])])
        mine = jnp.where(own_first, mine, mine[::-1])
        stats = lax.all_gather(mine, ('dp', 'tp'), axis=0, tiled=False)
        lse_max = jnp.max(stats[:, :, 0], axis=0)
        log_norm = lse_max + jnp.log(jnp.sum(jnp.exp(stats[:, :, 0] - lse_max[None]), axis=0))
        logp = jnp.sum(stats[:, :, 1], axis=0) - log_norm
        rows_used = info[0, 4, 0] + info[1, 4, 0]
        total_loss, d_logp = ppo_terms(logp, info[:, 2], info[:, 3], info[:, 1] / rows_used)

        dz, reduced = dx_reduced(z_own, z_other, to_mine(log_norm), to_mine(d_logp), to_mine(tgt_abs), w_shard, h_piece, gain_float[None], v_dev)
        gathered = lax.all_gather(reduced, 'tp', axis=0, tiled=False)
        d_head = head_grad(dz, x_own, x_other)
        d_gain = jnp.sum(gathered[:, piece:], axis=(0, 1))
        d_rows = gathered.reshape(n_tp // 2, 2, piece + 8, width)[:, :, :piece].reshape(n_tp // 2, 2, N_CHUNK, seg, width).transpose(2, 1, 0, 3, 4)
        d_hidden = (d_rows.reshape(n_tok, width) * inv_own).astype(BF16)
        return total_loss, d_hidden.reshape(row_count, seq_len, width), d_head, d_gain

    row_spec = P('dp', None)
    return jax.shard_map(local_step, mesh=mesh, in_specs=(P('dp', None, None), row_spec, row_spec, row_spec, row_spec, P(None), P('tp', None)), out_specs=(P(), P('dp', None, None), P(('tp', 'dp'), None), P(None)), check_vma=False)
```

time: 613 us -> 401 us (0.65)
  Pallas kernels: 0 us -> 313 us
  matrix products: 253 us -> 0 us
  waiting for transfers between devices: 242 us -> 0.06 us
  blocking collectives: 50.4 us -> 20.1 us
  other arithmetic: 49.7 us -> 40 us
  local copies, waits for them, and re-layouts: 2.74 us -> 11.2 us
    pallas_call x0 -> x4, Pallas kernels: none -> 313 us  [the longest x1 131 us: dx_reduced(): pl.pallas_call(functools.partial(dx_kernel, v_dev), grid=(N_CHUNK, v_dev...]
    dot_general x3 -> x0, matrix products: 253 us -> none  [the longest x1 86.3 us: local_step(): lax.dot_general(d_logits, w_half, (((0,), (0,)), ((), ())), preferred_ele...]
    reduce_scatter x1 -> x0, waiting for transfers between devices: 175 us -> none  [local_step(): lax.psum_scatter(dx_part, ('dp', 'tp'), scatter_dimension=0, tiled=True)]
    all_gather x1, waiting for transfers between devices: 67.2 us -> 0.01 us  [local_step(): h_all = lax.all_gather(h_piece, ('dp', 'tp'), axis=0, tiled=True)]
    psum x1 -> x0, blocking collectives: 30.9 us -> none  [local_step(): d_gain = lax.psum(jnp.sum(dx_mine * unit_rows, axis=0), ('dp', 'tp'))]
    reduce_sum x5 -> x8, other arithmetic: 24.5 us -> 6.93 us  [the longest x2 2.13 us: token_logits(): return (z_t, lse_loc, jnp.sum(zt, axis=0))]
    convert_element_type x3 -> x6, other arithmetic: 9.37 us -> 15.4 us  [the longest x2 10.4 us: norm_rows(): return (inv_rms, unit_rows, (unit_rows * gain_float).astype(BF16))]
  transfers between devices with their start and end apart: 3 -> 2, of which waited for: 2 -> 0; matrix products, arithmetic and copies ran while one was open for 16% -> 6% of each run, Pallas kernels for 0% -> 33%
where the time goes in v2:
time: 401 us; the launch traced here: 400 us
  Pallas kernels  313 us (78%)
  other arithmetic  40 us (10%)
  blocking collectives  20.1 us (5%)
  between operations  15.5 us (4%)
  local copies, waits for them, and re-layouts  11.2 us (3%)
    pallas_call x1, Pallas kernels, dx_reduced(): pl.pallas_call(functools.partial(dx_kernel, v_dev), grid=(N_CHUNK, v_dev...  131 us
    pallas_call x2, Pallas kernels, token_logits(): pl.pallas_call(functools.partial(logits_kernel, tb, 256), grid_spec=pltpu...  102 us
    pallas_call x1, Pallas kernels, head_grad(): pl.pallas_call(head_kernel, grid=(pl.cdiv(v_dev, vb),), in_specs=[pl.Bloc...  79.5 us
    all_gather x1, blocking collectives, local_step(): stats = lax.all_gather(mine, ('dp', 'tp'), axis=0, tiled=False)  13.6 us
    convert_element_type x2, other arithmetic, norm_rows(): return (inv_rms, unit_rows, (unit_rows * gain_float).astype(BF16))  10.4 us
  transfers between devices with their start and end apart: 2, of which 0 were waited for; matrix products, arithmetic and copies ran while one was open for 6% of the time, Pallas kernels for 33%

profile of v2, /device:TPU:0, one launch (start us, length us, event | category | flops | bytes accessed | tf_op | source)
XLA Modules:
  0.0 400.0 jit_solution(18164989132144428088)
XLA Ops:
  7.2 0.0 all-gather.7.cloned.1.call-start
  7.2 1.1 constant_dynamic-slice_fusion.1
  8.3 1.1 bitcast_convert_fusion.hp_ref
  9.4 0.0 all-gather.7.cloned.1.call-update
  9.5 0.0 all-gather.9.cloned.1.call-start
  9.5 0.8 reduce_sum.108
  10.3 0.6 fusion.22
  10.9 0.8 divide_bitcast_fusion
  11.7 0.7 convert_bitcast_fusion
  12.4 0.7 copy.38
  13.1 0.7 copy.39
  13.8 0.7 convert_element_type.67
  14.5 0.0 copy-start.3
  14.5 3.1 multiply_reduce_fusion
  17.6 0.6 add_rsqrt_fusion.1
  18.2 0.0 copy-done.3
  18.2 5.2 %fusion.4.x_ref = bf16[1024,2048]{1,0:T(8,128)(2,1)} fusion(f32[2048]{0:T(1024)S(1)} %convert_element_type.67, f32[1024]{0:T(1024)S(1)} %bitcast.167, bf16[2,512,2048]{2,1,0:T(8,128)(2,1)} %param.7), kind=kLoop, calls=%fused_computation.7 | loop fusion | flops 8388608 | bytes 8400896 | tf_op jit(solution)/shard_map/convert_element_type | solution.py:37
  23.4 0.6 stack_broadcast_in_dim.3
  24.1 6.5 %all-gather.3 = f32[2,5,1024]{2,1,0:T(8,128)S(1)} all-gather(f32[1,5,1024]{2,1,0:T(8,128)S(1)} %bitcast.165), channel_id=2, replica_groups=mesh['dp'=2,'tp'=8] {'dp'}, dimensions={0}, use_global_device_ids=true | all-gather | bytes 61440 | tf_op jit(solution)/shard_map/all_gather | solution.py:287
  30.6 0.0 copy-start
  30.6 0.6 copy-done
  31.2 0.6 slice_convert_fusion
  31.8 0.6 fusion.20
  32.4 51.2 %shard_map.102 = (f32[8016,1024]{1,0:T(8,128)}, f32[8,1024]{1,0:T(8,128)}, f32[8,1024]{1,0:T(8,128)}, f32[8,1024]{1,0:T(8,128)}) custom-call(s32[1]{0:T(128)} %bitcast.7.dp_ref, bf16[1024,2048]{1,0:T(8,128)(2,1)} %fusion.4.x_ref, bf16[16032,2048]{1,0:T(8,128)(2,1)} %w_ref.5, s32[1,1024]{1,0:T(1,128)} %get-tuple-element.44.tgt_ref), custom_call_target="tpu_custom_call" | custom-call | flops 33621540864 | bytes 65667072 | tf_op jit(solution)/shard_map/pallas_call | solution.py:62
  83.6 0.0 copy-start.4
  83.6 0.8 reduce_max.27
  84.4 1.4 reduce_sum.112
  85.8 1.3 fusion.24
  88.3 1.3 pad_add_fusion
  89.6 0.8 multiply_reduce_fusion.2
  90.4 0.6 log_add_fusion.2
  91.0 0.0 all-gather.7.cloned.1.call-done
  91.0 4.0 %fusion = f32[4,2,4,32]{3,0,1,2:T(4,128)S(1)} fusion(f32[2,4,2,4,32,2048]{5,4,3,2,1,0:T(8,128)} %bitcast.157, s32[]{:T(128)S(6)} %select_n.143), kind=kLoop, calls=%fused_computation.2 | loop fusion | flops 4193280 | bytes 8392708 | tf_op jit(solution)/shard_map/reduce_sum | solution.py:35
  95.0 0.0 copy-done.4
  95.0 5.2 %fusion.2 = bf16[4,2,4,32,2048]{4,3,0,1,2:T(8,128)(2,1)} fusion(f32[2048]{0:T(1024)S(1)} %copy-done.4, f32[4,2,4,32]{3,0,1,2:T(4,128)S(1)} %add_rsqrt_fusion, f32[2,4,2,4,32,2048]{5,4,3,2,1,0:T(8,128)} %bitcast.158, s32[]{:T(128)S(6)} %select_n.143), kind=kLoop, calls=%fused_computation.4 | loop fusion | flops 6291456 | bytes 12595204 | tf_op jit(solution)/shard_map/convert_element_type | solution.py:37
  100.3 51.2 %shard_map.103 = (f32[8016,1024]{1,0:T(8,128)}, f32[8,1024]{1,0:T(8,128)}, f32[8,1024]{1,0:T(8,128)}, f32[8,1024]{1,0:T(8,128)}) custom-call(s32[1]{0:T(128)} %bitcast.7.dp_ref, bf16[1024,2048]{1,0:T(8,128)(2,1)} %bitcast.162, bf16[16032,2048]{1,0:T(8,128)(2,1)} %w_ref.5, s32[1,1024]{1,0:T(1,128)} %get-tuple-element.43.tgt_ref), custom_call_target="tpu_custom_call" | custom-call | flops 33621540864 | bytes 65667072 | tf_op jit(solution)/shard_map/pallas_call | solution.py:62
  151.5 0.8 reduce_max.28
  152.2 0.8 multiply_reduce_fusion.1
  153.0 0.8 reduce_sum.115
  153.8 0.7 maximum_bitcast_fusion
  154.6 13.6 %all-gather.1 = f32[32,2,1024]{2,1,0:T(2,128)S(1)} all-gather(f32[2,2,1024]{2,1,0:T(2,128)S(1)} %reverse_select_fusion), channel_id=3, replica_groups=mesh['dp'=2,'tp'=8] {'dp','tp'}, dimensions={0}, use_global_device_ids=true | all-gather | bytes 278528 | tf_op jit(solution)/shard_map/all_gather | solution.py:309
  168.2 0.3 slice_reduce_fusion.2
  168.5 0.0 copy-start.1
  168.5 0.1 fusion.6
  168.6 0.5 copy-done.1
  169.1 0.8 fusion.9
  169.9 0.0 copy-start.2
  169.9 0.6 copy-done.2
  170.5 0.6 pad_maximum_fusion.2
  171.1 0.6 pad_maximum_fusion.1
  171.7 131.2 %shard_map.104 = (bf16[8016,2048]{1,0:T(8,128)(2,1)}, f32[136,2048]{1,0:T(8,128)}) custom-call(f32[8016,1024]{1,0:T(8,128)} %get-tuple-element.26.zo_ref, f32[8016,1024]{1,0:T(8,128)} %get-tuple-element.27.zr_ref, f32[1,2048]{1,0:T(1,128)} %bitcast.178, f32[1,2048]{1,0:T(1,128)} %bitcast.177, s32[1,2048]{1,0:T(1,128)} %bitcast.176, ...), custom_call_target="tpu_custom_call" | custom-call | flops 67243081728 | bytes 229834752 | tf_op jit(solution)/shard_map/pallas_call | solution.py:214
  302.9 0.0 all-gather.9.cloned.1.call-update
  302.9 1.4 fusion.14
  304.3 79.5 %shard_map.105 = f32[8016,2048]{1,0:T(8,128)} custom-call(bf16[8016,2048]{1,0:T(8,128)(2,1)} %get-tuple-element.29.dz_ref, bf16[8,128,2048]{2,1,0:T(8,128)(2,1)} %bitcast.161, bf16[8,128,2048]{2,1,0:T(8,128)(2,1)} %bitcast.163), custom_call_target="tpu_custom_call" | custom-call | flops 67243081728 | bytes 98500608 | tf_op jit(solution)/shard_map/pallas_call | solution.py:253
  383.8 0.0 all-gather.9.cloned.1.call-done
  383.8 4.0 slice.93
  387.8 0.0 copy-start.5
  387.8 1.1 copy.30
  388.9 1.7 slice_reduce_fusion
  390.6 0.0 copy-done.5
  390.6 2.5 multiply_convert_fusion
  (10 shorter events, 0.1 us)
Async XLA Ops:
  7.2 83.8 %all-gather.7.cloned.1.call-start = ((), (), s32[]{:S(2)}) async-start(), calls=%async_computation | async-start | bytes 17825792 | tf_op jit(solution)/shard_map/all_gather | solution.py:280
  9.5 374.3 %all-gather.9.cloned.1.call-start = ((), (), s32[]{:S(2)}) async-start(), calls=%async_computation.1 | async-start | bytes 10027008 | tf_op jit(solution)/shard_map/all_gather | solution.py:317
  14.5 3.7 copy-start.3
  30.6 0.6 copy-start
  83.6 11.4 %copy-start.4 = (f32[2048]{0:T(1024)S(1)}, f32[2048]{0:T(1024)}, u32[]{:S(2)}) copy-start(f32[2048]{0:T(1024)} %copy-done.3) | copy-start | bytes 24580
  168.5 0.6 copy-start.1
  169.9 0.6 copy-start.2
  387.8 2.8 copy-start.5
Sparse Core Ops, SparseCore 0:
  10.2 79.5 all-gather.6
  303.0 52.3 all-gather.8

commit v3 on v2

--- a/solution.py
+++ b/solution.py
@@ -37,12 +37,30 @@
     return inv_rms, unit_rows, (unit_rows * gain_float).astype(BF16)
 
 
-def logits_kernel(tb, sub, dp_ref, x_ref, w_ref, tgt_ref, z_ref, m_ref, s_ref, t_ref):
+def logits_kernel(tb, sub, dp_ref, h_ref, g_ref, w_ref, tgt_ref, z_ref, l_ref, y_ref, x_out, m_ref, s_ref, t_ref, xs, sem):
     v, t = pl.program_id(0), pl.program_id(1)
     rows = w_ref.shape[0]
+
+    def keep(i):
+        return pltpu.make_async_copy(xs.at[i], x_out.at[i], sem.at[i])
+
+    @pl.when(v == 0)
+    def _():
+        for i in range(tb // 128):
+            if len(h_ref.shape) == 2:
+                h = h_ref[i * 128:(i + 1) * 128, :].astype(F32)
+            else:
+                h = h_ref[0, :, i % 2, i // 2].reshape(128, h_ref.shape[-1])
+            xs[t, i * 128:(i + 1) * 128, :] = norm_rows(h, g_ref[...])[2]
+        keep(t).start()
+
+    @pl.when(v == 1)
+    def _():
+        keep(t).wait()
+
     for j in range(tb // sub):
         jc = pl.ds(pl.multiple_of(t * tb + j * sub, sub), sub)
-        z = lax.dot_general(w_ref[...], x_ref[j * sub:(j + 1) * sub, :], (((1,), (1,)), ((), ())), preferred_element_type=F32)
+        z = lax.dot_general(w_ref[...], xs[t, j * sub:(j + 1) * sub, :], (((1,), (1,)), ((), ())), preferred_element_type=F32)
         z_ref[:, j * sub:(j + 1) * sub] = z
         z3 = z.reshape(rows // 8, 8, sub)
         m_old = jnp.where(v == 0, -3e38, m_ref[:, jc])
@@ -54,26 +72,70 @@
         hit = lax.broadcasted_iota(jnp.int32, (rows, sub), 0) == tgt_ref[0:1, jc] - v * rows
         t_ref[:, jc] = t_old + jnp.sum(jnp.where(hit, z, 0.0).reshape(rows // 8, 8, sub), axis=0)
 
-
-def token_logits(x_rows, w_shard, tgt_rel, dp_i, v_dev):
-    n_tok, width = x_rows.shape
+    @pl.when((v == pl.num_programs(0) - 1) & (t == pl.num_programs(1) - 1))
+    def _():
+        m = m_ref[...]
+        m_loc = jnp.max(m, axis=0, keepdims=True)
+        l_ref[...] = m_loc + jnp.log(jnp.sum(s_ref[...] * jnp.exp(m - m_loc), axis=0, keepdims=True))
+        y_ref[...] = jnp.sum(t_ref[...], axis=0, keepdims=True)
+
+
+def token_logits(h_rows, gain_float, w_shard, tgt_rel, dp_i, v_dev):
+    n_tok, width = tgt_rel.shape[1], w_shard.shape[1]
     tb, n_v = 512, v_dev // V_BLK
-    full = pl.BlockSpec((8, n_tok), lambda v, t, d: (0, 0))
-    z_t, m, s, zt = pl.pallas_call(
+    n_t = n_tok // tb
+    full = pl.BlockSpec((1, n_tok), lambda v, t, d: (0, 0))
+    if h_rows.ndim == 2:
+        h_spec = pl.BlockSpec((tb, width), lambda v, t, d: (jnp.where(v == 0, t, n_t - 1), 0))
+    else:
+        per = N_CHUNK // n_t
+        h_spec = pl.BlockSpec((1, h_rows.shape[1], 2, per, h_rows.shape[4], width), lambda v, t, d: (1 - d[0], 0, 0, jnp.where(v == 0, t, n_t - 1), 0, 0))
+    z_t, lse_loc, zt_loc, x_rows = pl.pallas_call(
         functools.partial(logits_kernel, tb, 256),
         grid_spec=pltpu.PrefetchScalarGridSpec(
-            num_scalar_prefetch=1, grid=(n_v, n_tok // tb),
-            in_specs=[pl.BlockSpec((tb, width), lambda v, t, d: (t, 0)),
+            num_scalar_prefetch=1, grid=(n_v, n_t),
+            in_specs=[h_spec, pl.BlockSpec((1, width), lambda v, t, d: (0, 0)),
                       pl.BlockSpec((V_BLK, width), lambda v, t, d: (d[0] * n_v + v, 0)),
                       pl.BlockSpec((1, n_tok), lambda v, t, d: (0, 0))],
-            out_specs=[pl.BlockSpec((V_BLK, tb), lambda v, t, d: (v, t)), full, full, full]),
-        out_shape=[jax.ShapeDtypeStruct((v_dev, n_tok), F32)] + [jax.ShapeDtypeStruct((8, n_tok), F32)] * 3,
+            out_specs=[pl.BlockSpec((V_BLK, tb), lambda v, t, d: (v, t)), full, full, pl.BlockSpec(memory_space=pl.ANY)],
+            scratch_shapes=[pltpu.VMEM((8, n_tok), F32)] * 3 + [pltpu.VMEM((n_t, tb, width), BF16), pltpu.SemaphoreType.DMA((n_t,))]),
+        out_shape=[jax.ShapeDtypeStruct((v_dev, n_tok), F32)] + [jax.ShapeDtypeStruct((1, n_tok), F32)] * 2 + [jax.ShapeDtypeStruct((n_t, tb, width), BF16)],
         compiler_params=pltpu.CompilerParams(vmem_limit_bytes=VMEM_MAX),
         cost_estimate=pl.CostEstimate(flops=2 * v_dev * n_tok * width, bytes_accessed=v_dev * n_tok * 4 + v_dev * width * 2, transcendentals=v_dev * n_tok),
-    )(dp_i.reshape(1), x_rows, w_shard, tgt_rel)
-    m_loc = jnp.max(m, axis=0)
-    lse_loc = m_loc + jnp.log(jnp.sum(s * jnp.exp(m - m_loc[None]), axis=0))
-    return z_t, lse_loc, jnp.sum(zt, axis=0)
+    )(dp_i.reshape(1), h_rows, gain_float, w_shard, tgt_rel)
+    return z_t, lse_loc[0], zt_loc[0], x_rows
+
+
+def stats_kernel(mine_ref, out_ref, got, snd, rcv):
+    dp, tp = lax.axis_index('dp'), lax.axis_index('tp')
+    core, xx, yy = tp % 2, (tp // 2) % 2, tp // 4
+    me = dp * 8 + tp
+
+    def peer(r):
+        flip = lambda a, bit: 1 - a if (r >> bit) & 1 else a
+        return (flip(dp, 3), flip(yy, 2) * 4 + flip(xx, 1) * 2 + flip(core, 0))
+
+    barrier = pltpu.get_barrier_semaphore()
+    for r in range(1, 16):
+        pl.semaphore_signal(barrier, inc=1, device_id=peer(r), device_id_type=MESH)
+    pl.semaphore_wait(barrier, 15)
+    copies = [pltpu.make_async_remote_copy(mine_ref, got.at[me], snd.at[r], rcv.at[r], device_id=peer(r), device_id_type=MESH) for r in range(1, 16)]
+    for copy in copies:
+        copy.start()
+    got[me] = mine_ref[...]
+    for copy in copies:
+        copy.wait()
+    out_ref[...] = got[...]
+
+
+def exchange_stats(mine):
+    vmem = pl.BlockSpec(memory_space=pltpu.VMEM)
+    return pl.pallas_call(
+        stats_kernel, in_specs=[vmem], out_specs=vmem,
+        out_shape=jax.ShapeDtypeStruct((16,) + mine.shape, F32),
+        scratch_shapes=[pltpu.VMEM((16,) + mine.shape, F32), pltpu.SemaphoreType.DMA((16,)), pltpu.SemaphoreType.DMA((16,))],
+        compiler_params=pltpu.CompilerParams(collective_id=1, has_side_effects=True),
+    )(mine)
 
 
 def dx_kernel(v_dev, zo_ref, zr_ref, lse_ref, dl_ref, tgt_ref, w_ref, hp_ref, g_ref, dz_ref, out_ref,
@@ -148,7 +210,7 @@
         unit_rows = h_rows * inv_rms
         dg[...] += jnp.sum((d_act * unit_rows).reshape(4, 8, d_act.shape[1]), axis=0)
         d_unit = d_act * g_ref[...]
-        out_ref[rows, :] = d_unit - unit_rows * jnp.mean(d_unit * unit_rows, axis=-1, keepdims=True)
+        out_ref[pl.ds(pl.multiple_of(j * 40, 8), 32), :] = d_unit - unit_rows * jnp.mean(d_unit * unit_rows, axis=-1, keepdims=True)
 
     @pl.when((k == 0) & (v == 0))
     def _():
@@ -201,7 +263,7 @@
         last = pltpu.make_async_remote_copy(dg, dg_got, snd_g, rcv_g, device_id=by_z, device_id_type=MESH)
         last.start()
         last.wait()
-        out_ref[pl.ds(128, 8), :] = dg[...] + dg_got[...]
+        out_ref[pl.ds(N_CHUNK * 40 - 8, 8), :] = dg[...] + dg_got[...]
 
 
 def dx_reduced(z_own, z_other, lse, d_logp, tgt, w_shard, h_piece, gain_float, v_dev):
@@ -219,8 +281,8 @@
                   pl.BlockSpec((V_BLK, width), lambda k, v: (lax.axis_index('dp') * (v_dev // V_BLK) + v, 0)),
                   pl.BlockSpec(h_piece.shape, lambda k, v: (0, 0), pipeline_mode=pl.Buffered(1)),
                   pl.BlockSpec((1, width), lambda k, v: (0, 0))],
-        out_specs=[pl.BlockSpec((V_BLK, tb), lambda k, v: (v, k)), pl.BlockSpec((h_piece.shape[0] + 8, width), lambda k, v: (0, 0), pipeline_mode=pl.Buffered(1))],
-        out_shape=[jax.ShapeDtypeStruct((v_dev, n_all), BF16), jax.ShapeDtypeStruct((h_piece.shape[0] + 8, width), F32)],
+        out_specs=[pl.BlockSpec((V_BLK, tb), lambda k, v: (v, k)), pl.BlockSpec((N_CHUNK * 40, width), lambda k, v: (0, 0), pipeline_mode=pl.Buffered(1))],
+        out_shape=[jax.ShapeDtypeStruct((v_dev, n_all), BF16), jax.ShapeDtypeStruct((N_CHUNK * 40, width), F32)],
         scratch_shapes=[vm(2, 2, 2, 2, 2, 32, width), vm(2, 2, 2, 2, 32, width)]
         + [vm(2, 2, 2, 32, n) for n in sizes] + [vm(2, 2, 32, n) for n in sizes] + [vm(2, 32, n) for n in sizes]
         + [vm(2, 2, 32, n) for n in sizes] + [vm(2, 32, n) for n in sizes]
@@ -248,8 +310,8 @@
 
 def head_grad(dz, x_own, x_other):
     v_dev, n_all = dz.shape
-    width = x_own.shape[1]
-    vb, groups = 512, n_all // 256
+    width = x_own.shape[-1]
+    vb, groups = 576, n_all // 256
     return pl.pallas_call(
         head_kernel, grid=(pl.cdiv(v_dev, vb),),
         in_specs=[pl.BlockSpec((vb, n_all), lambda v: (v, 0)), pl.BlockSpec(memory_space=pl.ANY), pl.BlockSpec(memory_space=pl.ANY)],
@@ -261,6 +323,35 @@
     )(dz, x_own.reshape(groups, 128, width), x_other.reshape(groups, 128, width))
 
 
+def finish_kernel(u_ref, h_ref, dh_ref, dg_ref):
+    seg = u_ref.shape[3] - 8
+    half = h_ref.shape[0] // 2
+    for core in range(2):
+        rows = pl.ds(core * half, half)
+        h = h_ref[rows, :].astype(F32)
+        inv_rms = lax.rsqrt(jnp.mean(h * h, axis=-1, keepdims=True) + EPSILON)
+        dh_ref[rows, :] = (u_ref[:, core, 0, :seg].reshape(half, h.shape[1]) * inv_rms).astype(BF16)
+
+    @pl.when(pl.program_id(0) == N_CHUNK - 1)
+    def _():
+        total = u_ref[0, 0, 0, seg:]
+        for i in range(1, u_ref.shape[0] * 2):
+            total = total + u_ref[i // 2, i % 2, 0, seg:]
+        dg_ref[...] = jnp.sum(total, axis=0, keepdims=True)
+
+
+def finish(gathered, h_flat):
+    n_yx, n_core, n_k, rows, width = gathered.shape
+    n_tok = h_flat.shape[0]
+    return pl.pallas_call(
+        finish_kernel, grid=(n_k,),
+        in_specs=[pl.BlockSpec((n_yx, n_core, 1, rows, width), lambda k: (0, 0, k, 0, 0)), pl.BlockSpec((n_tok // n_k, width), lambda k: (k, 0))],
+        out_specs=[pl.BlockSpec((n_tok // n_k, width), lambda k: (k, 0)), pl.BlockSpec((1, width), lambda k: (0, 0))],
+        out_shape=[jax.ShapeDtypeStruct((n_tok, width), BF16), jax.ShapeDtypeStruct((1, width), F32)],
+        compiler_params=pltpu.CompilerParams(vmem_limit_bytes=VMEM_MAX),
+    )(gathered, h_flat)
+
+
 def solution(mesh):
     n_dp, n_tp = mesh.shape['dp'], mesh.shape['tp']
 
@@ -292,21 +383,17 @@
             return jnp.stack([jnp.where(dp_i == 0, b[0], b[1]), jnp.where(dp_i == 0, b[1], b[0])], axis=1).reshape(1, n_all)
 
         v_base = (tp_i * n_dp + dp_i) * v_dev
-        tgt_own = lax.dynamic_index_in_dim(tgt_abs, dp_i, 0, keepdims=True) - v_base
+        tgt_own = targets.reshape(1, n_tok) - v_base
         tgt_other = lax.dynamic_index_in_dim(tgt_abs, 1 - dp_i, 0, keepdims=True) - v_base
 
-        inv_own, _, x_own = norm_rows(h_flat.astype(F32), gain_float)
-        x_own = lax.optimization_barrier(x_own)
-        z_own, lse_own, zt_own = token_logits(x_own, w_shard, tgt_own, dp_i, v_dev)
+        z_own, lse_own, zt_own, x_own = token_logits(h_flat, gain_float[None], w_shard, tgt_own, dp_i, v_dev)
         h_all, lse_own, zt_own = lax.optimization_barrier((h_all, lse_own, zt_own))
-        h_other = lax.dynamic_index_in_dim(h_all.reshape(n_dp, n_tp // 2, 2, N_CHUNK, seg, width), 1 - dp_i, 0, keepdims=False)
-        x_other = norm_rows(h_other, gain_float)[2].transpose(2, 1, 0, 3, 4).reshape(n_tok, width)
-        z_other, lse_other, zt_other = token_logits(x_other, w_shard, tgt_other, dp_i, v_dev)
+        z_other, lse_other, zt_other, x_other = token_logits(h_all.reshape(n_dp, n_tp // 2, 2, N_CHUNK, seg, width), gain_float[None], w_shard, tgt_other, dp_i, v_dev)
 
         own_first = dp_i == 0
         mine = jnp.stack([jnp.stack([lse_own, zt_own]), jnp.stack([lse_other, zt_other])])
         mine = jnp.where(own_first, mine, mine[::-1])
-        stats = lax.all_gather(mine, ('dp', 'tp'), axis=0, tiled=False)
+        stats = exchange_stats(mine.reshape(4 * n_tok // 128, 128)).reshape(n_dp * n_tp, 2, 2, n_tok)
         lse_max = jnp.max(stats[:, :, 0], axis=0)
         log_norm = lse_max + jnp.log(jnp.sum(jnp.exp(stats[:, :, 0] - lse_max[None]), axis=0))
         logp = jnp.sum(stats[:, :, 1], axis=0) - log_norm
@@ -316,10 +403,8 @@
         dz, reduced = dx_reduced(z_own, z_other, to_mine(log_norm), to_mine(d_logp), to_mine(tgt_abs), w_shard, h_piece, gain_float[None], v_dev)
         gathered = lax.all_gather(reduced, 'tp', axis=0, tiled=False)
         d_head = head_grad(dz, x_own, x_other)
-        d_gain = jnp.sum(gathered[:, piece:], axis=(0, 1))
-        d_rows = gathered.reshape(n_tp // 2, 2, piece + 8, width)[:, :, :piece].reshape(n_tp // 2, 2, N_CHUNK, seg, width).transpose(2, 1, 0, 3, 4)
-        d_hidden = (d_rows.reshape(n_tok, width) * inv_own).astype(BF16)
-        return total_loss, d_hidden.reshape(row_count, seq_len, width), d_head, d_gain
+        d_hidden, d_gain = finish(gathered.reshape(n_tp // 2, 2, N_CHUNK, seg + 8, width), h_flat)
+        return total_loss, d_hidden.reshape(row_count, seq_len, width), d_head, d_gain[0]
 
     row_spec = P('dp', None)
     return jax.shard_map(local_step, mesh=mesh, in_specs=(P('dp', None, None), row_spec, row_spec, row_spec, row_spec, P(None), P('tp', None)), out_specs=(P(), P('dp', None, None), P(('tp', 'dp'), None), P(None)), check_vma=False)

time: 401 us -> 387 us (0.965)
  other arithmetic: 40 us -> 13.7 us
  Pallas kernels: 313 us -> 334 us
  blocking collectives: 20.1 us -> 6.1 us
  waiting for transfers between devices: 0.06 us -> 9.88 us
  local copies, waits for them, and re-layouts: 11.2 us -> 7.05 us
    pallas_call x0 -> x2, Pallas kernels: none -> 16.8 us  [the longest x1 9.19 us: exchange_stats(): pl.pallas_call(stats_kernel, in_specs=[vmem], out_specs=vmem, out_shape=j...]
    convert_element_type x4 -> x0, other arithmetic: 13.7 us -> none  [the longest x2 10.4 us: norm_rows(): return (inv_rms, unit_rows, (unit_rows * gain_float).astype(BF16))]
    all_gather x1 -> x0, blocking collectives: 13.6 us -> none  [local_step(): stats = lax.all_gather(mine, ('dp', 'tp'), axis=0, tiled=False)]
    reduce_sum x7 -> x0, other arithmetic: 12.5 us -> none  [the longest x2 7.09 us: norm_rows(): jnp.mean(h_float * h_float, axis=-1, keepdims=True) + EPSILON]
    all_gather x1, waiting for transfers between devices: 0.01 us -> 9.82 us  [local_step(): h_all = lax.all_gather(h_piece, ('dp', 'tp'), axis=0, tiled=True)]
    pallas_call x2, Pallas kernels: 102 us -> 107 us  [token_logits(): pl.pallas_call(functools.partial(logits_kernel, tb, 256), grid_spec=pltpu...]
  transfers between devices with their start and end apart: 2 -> 2, of which waited for: 0 -> 1; matrix products, arithmetic and copies ran while one was open for 6% -> 3% of each run, Pallas kernels for 33% -> 34%
where the time goes in v3:
time: 387 us; the launch traced here: 386 us
  Pallas kernels  334 us (86%)
  between operations  15.5 us (4%)
  other arithmetic  13.7 us (4%)
  waiting for transfers between devices  9.88 us (3%)
  local copies, waits for them, and re-layouts  7.05 us (2%)
  blocking collectives  6.1 us (2%)
    pallas_call x1, Pallas kernels, dx_reduced(): pl.pallas_call(functools.partial(dx_kernel, v_dev), grid=(N_CHUNK, v_dev...  132 us
    pallas_call x2, Pallas kernels, token_logits(): pl.pallas_call(functools.partial(logits_kernel, tb, 256), grid_spec=pltpu...  107 us
    pallas_call x1, Pallas kernels, head_grad(): pl.pallas_call(head_kernel, grid=(pl.cdiv(v_dev, vb),), in_specs=[pl.Bloc...  78.5 us
    all_gather x1, waiting for transfers between devices, local_step(): h_all = lax.all_gather(h_piece, ('dp', 'tp'), axis=0, tiled=True)  9.82 us
    pallas_call x1, Pallas kernels, exchange_stats(): pl.pallas_call(stats_kernel, in_specs=[vmem], out_specs=vmem, out_shape=j...  9.19 us
  transfers between devices with their start and end apart: 2, of which 1 were waited for; matrix products, arithmetic and copies ran while one was open for 3% of the time, Pallas kernels for 34%

profile of v3, /device:TPU:0, one launch (start us, length us, event | category | flops | bytes accessed | tf_op | source)
XLA Modules:
  0.0 386.5 jit_solution(16835555120537963838)
XLA Ops:
  7.2 0.0 all-gather.6.cloned.1.call-start
  7.2 1.1 constant_dynamic-slice_fusion
  8.3 1.1 bitcast_convert_fusion.hp_ref
  9.4 0.0 all-gather.6.cloned.1.call-update
  9.5 0.0 all-gather.8.cloned.1.call-start
  9.5 0.8 subtract_bitcast_fusion.1
  10.3 0.6 copy.36
  10.9 1.3 broadcast_in_dim.15
  12.2 0.8 reduce_sum.45
  13.0 0.6 fusion.17
  13.6 0.8 divide_bitcast_fusion
  14.4 0.7 copy.34
  15.1 0.7 copy.35
  15.7 0.6 stack_broadcast_in_dim.3
  16.4 6.1 %all-gather.2 = f32[2,5,1024]{2,1,0:T(8,128)S(1)} all-gather(f32[1,5,1024]{2,1,0:T(8,128)S(1)} %bitcast.135), channel_id=2, replica_groups=mesh['dp'=2,'tp'=8] {'dp'}, dimensions={0}, use_global_device_ids=true | all-gather | bytes 61440 | tf_op jit(solution)/shard_map/all_gather | solution.py:378
  22.5 0.5 fusion.18
  24.4 0.6 slice_convert_fusion
  25.0 0.6 fusion.15
  25.6 0.6 pad_add_fusion
  26.2 53.5 %shard_map.102 = (f32[8016,1024]{1,0:T(8,128)}, f32[1,1024]{1,0:T(1,128)}, f32[1,1024]{1,0:T(1,128)}, bf16[2,512,2048]{2,1,0:T(8,128)(2,1)}) custom-call(s32[1]{0:T(128)} %bitcast.7.dp_ref, bf16[1024,2048]{1,0:T(8,128)(2,1)} %bitcast.133, f32[1,2048]{1,0:T(1,128)} %bitcast.140, bf16[16032,2048]{1,0:T(8,128)(2,1)} %w_ref.5, s32[1,1024]{1,0:T(1,128)} %bitcast.148), custom_call_target="tpu_custom_call" | custom-call | flops 33621540864 | bytes 65667072 | tf_op jit(solution)/shard_map/pallas_call | solution.py:93
  79.7 9.8 %all-gather.6.cloned.1.call-done = f32[2048,2048]{1,0:T(8,128)} async-done(((f32[128,2048]{1,0:T(8,128)}), f32[2048,2048]{1,0:T(8,128)}) %all-gather.6.cloned.1.call-update) | async-done | bytes 16777232 | tf_op jit(solution)/shard_map/all_gather | solution.py:371
  89.5 1.3 maximum_bitcast_fusion
  90.8 53.9 %shard_map.103 = (f32[8016,1024]{1,0:T(8,128)}, f32[1,1024]{1,0:T(1,128)}, f32[1,1024]{1,0:T(1,128)}, bf16[2,512,2048]{2,1,0:T(8,128)(2,1)}) custom-call(s32[1]{0:T(128)} %bitcast.7.dp_ref, f32[2,4,2,4,32,2048]{5,4,3,2,1,0:T(8,128)} %bitcast.149, f32[1,2048]{1,0:T(1,128)} %bitcast.141, bf16[16032,2048]{1,0:T(8,128)(2,1)} %w_ref.5, ...), custom_call_target="tpu_custom_call" | custom-call | flops 33621540864 | bytes 65667072 | tf_op jit(solution)/shard_map/pallas_call | solution.py:93
  144.7 0.7 maximum_bitcast_fusion.1
  145.4 0.7 pad_maximum_fusion
  146.1 0.6 reshape.233.mine_ref
  146.7 9.2 %shard_map.104 = f32[16,32,128]{2,1,0:T(8,128)} custom-call(f32[32,128]{1,0:T(8,128)} %reshape.233.mine_ref), custom_call_target="tpu_custom_call" | custom-call | tf_op jit(solution)/shard_map/pallas_call | solution.py:133
  155.9 1.1 reshape.234
  157.0 0.3 slice_reduce_fusion.1
  157.3 0.0 copy-start
  157.3 0.1 fusion.1
  157.4 0.5 copy-done
  157.9 0.8 fusion.4
  158.7 0.0 copy-start.1
  158.7 0.6 copy-done.1
  159.3 0.6 pad_maximum_fusion.2
  159.9 0.6 pad_maximum_fusion.1
  160.5 131.5 %shard_map.105 = (bf16[8016,2048]{1,0:T(8,128)(2,1)}, f32[160,2048]{1,0:T(8,128)}) custom-call(f32[8016,1024]{1,0:T(8,128)} %get-tuple-element.26.zo_ref, f32[8016,1024]{1,0:T(8,128)} %get-tuple-element.27.zr_ref, f32[1,2048]{1,0:T(1,128)} %bitcast.145, f32[1,2048]{1,0:T(1,128)} %bitcast.144, s32[1,2048]{1,0:T(1,128)} %bitcast.143, ...), custom_call_target="tpu_custom_call" | custom-call | flops 67243081728 | bytes 229834752 | tf_op jit(solution)/shard_map/pallas_call | solution.py:276
  292.0 0.0 all-gather.8.cloned.1.call-update
  292.1 1.4 fusion.9
  293.5 78.5 %shard_map.107 = f32[8016,2048]{1,0:T(8,128)} custom-call(bf16[8016,2048]{1,0:T(8,128)(2,1)} %get-tuple-element.30.dz_ref, bf16[8,128,2048]{2,1,0:T(8,128)(2,1)} %bitcast.152, bf16[8,128,2048]{2,1,0:T(8,128)(2,1)} %bitcast.153), custom_call_target="tpu_custom_call" | custom-call | flops 67243081728 | bytes 98500608 | tf_op jit(solution)/shard_map/pallas_call | solution.py:315
  372.0 0.0 all-gather.8.cloned.1.call-done
  372.1 7.6 %shard_map.106 = (bf16[1024,2048]{1,0:T(8,128)(2,1)}, f32[1,2048]{1,0:T(1,128)}) custom-call(f32[4,2,4,40,2048]{4,3,2,1,0:T(8,128)} %bitcast.131, bf16[1024,2048]{1,0:T(8,128)(2,1)} %bitcast.134), custom_call_target="tpu_custom_call" | custom-call | tf_op jit(solution)/shard_map/pallas_call | solution.py:346
  (5 shorter events, 0.1 us)
Async XLA Ops:
  7.2 82.3 %all-gather.6.cloned.1.call-start = ((), (), s32[]{:S(2)}) async-start(), calls=%async_computation | async-start | bytes 17825792 | tf_op jit(solution)/shard_map/all_gather | solution.py:371
  9.5 362.6 %all-gather.8.cloned.1.call-start = ((), (), s32[]{:S(2)}) async-start(), calls=%async_computation.1 | async-start | bytes 11796480 | tf_op jit(solution)/shard_map/all_gather | solution.py:404
  157.3 0.6 copy-start
  158.7 0.6 copy-start.1
Sparse Core Ops, SparseCore 0:
  10.2 79.2 all-gather.5
  292.2 58.6 all-gather.7
